TPU v7x, 32 devices: a whole 2x2x4 slice. The times are simulated.
32 devices in a mesh: dp: 8 (over z, core), tensor: 4 (over y, x).
Axes of the slice: x: 2, y: 2, z: 4, core: 2. Of those that a mesh axis runs over, the one named last changes fastest.
Arguments:
- inputs: bfloat16 [8192, 2048], P(('dp', 'tensor'))
- doc_lengths: int32 [8, 4], P('dp'), may hold values from 0 to 1024, as said below
- attn_gain: bfloat16 [2048], P('dp'), may hold values from 0.099609375 to 1.8984375
- w_query: bfloat16 [2048, 2048], P('dp', 'tensor')
- w_key: bfloat16 [2048, 512], P('dp', 'tensor')
- value_weight: bfloat16 [2048, 512], P('dp', 'tensor'), may hold values from -0.125 to 0.125
- w_output: bfloat16 [2048, 2048], P('tensor', 'dp'), may hold values from -0.5 to 0.5
- mlp_gain: bfloat16 [2048], P('dp'), may hold values from 0.099609375 to 1.8984375
- w_gate: bfloat16 [2048, 8192], P('dp', 'tensor'), may hold values from -0.125 to 0.125
- w_up: bfloat16 [2048, 8192], P('dp', 'tensor'), may hold values from -0.125 to 0.125
- w_down: bfloat16 [8192, 2048], P('tensor', 'dp'), may hold values from -0.125 to 0.125
- out_grad: bfloat16 [8192, 2048], P(('dp', 'tensor')), may hold values from -6 to 6
Outputs:
- output: float32 [8192, 2048], P(('dp', 'tensor'))
- input_grad: float32 [8192, 2048], P(('dp', 'tensor'))
- attn_gain_grad: float32 [2048], P('dp')
- w_query_grad: float32 [2048, 2048], P('dp', 'tensor')
- w_key_grad: float32 [2048, 512], P('dp', 'tensor')
- w_value_grad: float32 [2048, 512], P('dp', 'tensor')
- w_output_grad: float32 [2048, 2048], P('tensor', 'dp')
- mlp_gain_grad: float32 [2048], P('dp')
- w_gate_grad: float32 [2048, 8192], P('dp', 'tensor')
- w_up_grad: float32 [2048, 8192], P('dp', 'tensor')
- w_down_grad: float32 [8192, 2048], P('tensor', 'dp')
Inputs may be any that keep to these rules, and one draw needn't show every extreme that they name: `doc_lengths`: row r lists the lengths of the 4 documents packed back to back from the first slot of dp index r; a row sums to at most 1024, zero lengths occur, and in every draw some row holds a single document of 1024 tokens.
All inputs are finite; a program needn't handle non-finite values.
Results may differ from a plain program's by a relative error of at most 0.017.
The roundings to bfloat16 on the way count: a program that leaves them out, or rounds other values in their place, can miss the bound.
Values may be sent and summed in bfloat16 or wider, within the bound.
A program may use at most 256 MiB of HBM per device.

v0:
```python
import jax
import jax.numpy as jnp
from jax import lax
from jax.sharding import PartitionSpec as P

HEAD_SIZE = 64
QBLK = 512
epsilon = 1e-05
rope_base = 500000.0


def layout(lengths, total_rows):
    row_index = jnp.arange(total_rows, dtype=jnp.int32)
    doc_ends = jnp.cumsum(lengths)
    passed = doc_ends[None, :] <= row_index[:, None]
    document_segment = jnp.sum(passed.astype(jnp.int32), axis=1)
    doc_start = jnp.sum(jnp.where(passed, lengths[None, :], 0), axis=1)
    positions = (row_index - doc_start).astype(jnp.float32)
    valid_rows = (document_segment < lengths.shape[0]).astype(jnp.float32)
    return (document_segment, positions, valid_rows)


def rope_tables(positions, head_dim):
    half_dim = head_dim // 2
    inverse_freq = rope_base ** (-(jnp.arange(half_dim, dtype=jnp.float32) * 2.0 / head_dim))
    angles = positions[:, None] * inverse_freq[None, :]
    return (jnp.cos(angles)[:, None, :], jnp.sin(angles)[:, None, :])


def rotate(tensor, cosine, sine_part, direction):
    half_dim = tensor.shape[-1] // 2
    first_half = tensor[..., :half_dim]
    second_half = tensor[..., half_dim:]
    return jnp.concatenate(
        [
            first_half * cosine - direction * second_half * sine_part,
            second_half * cosine + direction * first_half * sine_part,
        ],
        axis=-1,
    )


def rms_stats(hidden):
    scale_row = lax.rsqrt(jnp.mean(hidden * hidden, axis=-1, keepdims=True) + epsilon)
    return (scale_row, hidden * scale_row)


def norm_backward(grad_normed, unit_rows, scale_row, gain_wide):
    scaled = grad_normed * gain_wide
    return scale_row * (scaled - unit_rows * jnp.mean(scaled * unit_rows, axis=-1, keepdims=True))


def block_mask(document_segment, first_row, block_rows):
    row_index = jnp.arange(document_segment.shape[0], dtype=jnp.int32)
    query_rows = first_row + jnp.arange(block_rows, dtype=jnp.int32)
    query_segment = lax.dynamic_slice_in_dim(document_segment, first_row, block_rows, 0)
    return (query_segment[:, None] == document_segment[None, :]) & (
        row_index[None, :] <= query_rows[:, None]
    )


def attention_forward(queries, keys_rot, values, document_segment, block_rows):
    total_rows, kv_heads, group_size, head_dim = queries.shape
    score_scale = head_dim ** (-0.5)

    def one_block(block_index):
        first_row = block_index * block_rows
        query_block = lax.dynamic_slice_in_dim(queries, first_row, block_rows, 0)
        allowed = block_mask(document_segment, first_row, block_rows)
        scores = (
            jnp.einsum("qkgd,skd->kgqs", query_block, keys_rot, preferred_element_type=jnp.float32)
            * score_scale
        )
        scores = jnp.where(allowed, scores, -jnp.inf)
        row_max = jnp.max(scores, axis=-1, keepdims=True)
        log_total = row_max + jnp.log(jnp.sum(jnp.exp(scores - row_max), axis=-1, keepdims=True))
        weights = jnp.exp(scores - log_total).astype(jnp.bfloat16)
        attended = jnp.einsum("kgqs,skd->qkgd", weights, values, preferred_element_type=jnp.float32)
        return (attended.astype(jnp.bfloat16), log_total[..., 0])

    attended, log_total = lax.map(one_block, jnp.arange(total_rows // block_rows, dtype=jnp.int32))
    return (attended.reshape(total_rows, kv_heads, group_size, head_dim), log_total)


def attention_backward(
    queries, keys_rot, values, attended, grad_attended, log_total, document_segment, block_rows
):
    total_rows, kv_heads, group_size, head_dim = queries.shape
    score_scale = head_dim ** (-0.5)

    def one_block(running, block_index):
        key_grad, value_grad = running
        first_row = block_index * block_rows
        query_block = lax.dynamic_slice_in_dim(queries, first_row, block_rows, 0)
        block_gradient = lax.dynamic_slice_in_dim(grad_attended, first_row, block_rows, 0)
        out_block = lax.dynamic_slice_in_dim(attended, first_row, block_rows, 0)
        allowed = block_mask(document_segment, first_row, block_rows)
        scores = (
            jnp.einsum("qkgd,skd->kgqs", query_block, keys_rot, preferred_element_type=jnp.float32)
            * score_scale
        )
        scores = jnp.where(allowed, scores, -jnp.inf)
        prob_full = jnp.exp(scores - log_total[block_index][..., None])
        weights = prob_full.astype(jnp.bfloat16)
        value_grad = value_grad + jnp.einsum(
            "kgqs,qkgd->skd", weights, block_gradient, preferred_element_type=jnp.float32
        )
        grad_probs = jnp.einsum(
            "qkgd,skd->kgqs", block_gradient, values, preferred_element_type=jnp.float32
        )
        row_delta = jnp.einsum(
            "qkgd,qkgd->kgq", block_gradient, out_block, preferred_element_type=jnp.float32
        )
        grad_scores = (prob_full * (grad_probs - row_delta[..., None])).astype(jnp.bfloat16)
        query_grad = (
            jnp.einsum("kgqs,skd->qkgd", grad_scores, keys_rot, preferred_element_type=jnp.float32)
            * score_scale
        )
        key_grad = (
            key_grad
            + jnp.einsum(
                "kgqs,qkgd->skd", grad_scores, query_block, preferred_element_type=jnp.float32
            )
            * score_scale
        )
        return ((key_grad, value_grad), query_grad)

    zero_keys = jnp.zeros((total_rows, kv_heads, head_dim), jnp.float32)
    (key_grad, value_grad), query_grad = lax.scan(
        one_block, (zero_keys, zero_keys), jnp.arange(total_rows // block_rows, dtype=jnp.int32)
    )
    return (query_grad.reshape(total_rows, kv_heads * group_size, head_dim), key_grad, value_grad)


def attn_params(attn_gain, w_query, w_key, value_weight, w_output):
    return (
        lax.all_gather(attn_gain, "dp", axis=0, tiled=True),
        lax.all_gather(w_query, "dp", axis=0, tiled=True),
        lax.all_gather(w_key, "dp", axis=0, tiled=True),
        lax.all_gather(value_weight, "dp", axis=0, tiled=True),
        lax.all_gather(w_output, "dp", axis=1, tiled=True),
    )


def mlp_params(mlp_gain, w_gate, w_up, w_down):
    return (
        lax.all_gather(mlp_gain, "dp", axis=0, tiled=True),
        lax.all_gather(w_gate, "dp", axis=0, tiled=True),
        lax.all_gather(w_up, "dp", axis=0, tiled=True),
        lax.all_gather(w_down, "dp", axis=1, tiled=True),
    )


def per_device(
    inputs,
    doc_lengths,
    attn_gain,
    w_query,
    w_key,
    value_weight,
    w_output,
    mlp_gain,
    w_gate,
    w_up,
    w_down,
    out_grad,
):
    tensor_count = lax.axis_size("tensor")
    tensor_rank = lax.axis_index("tensor")
    own_rows = inputs.shape[0]
    total_rows = own_rows * tensor_count
    document_segment, positions, valid_rows = layout(doc_lengths[0], total_rows)
    valid_own = lax.dynamic_slice_in_dim(valid_rows, tensor_rank * own_rows, own_rows, 0)[:, None]
    cosine, sine_part = rope_tables(positions, HEAD_SIZE)
    gain_one, full_query, full_key, full_value, full_output = attn_params(
        attn_gain, w_query, w_key, value_weight, w_output
    )
    gain_two, full_gate, full_up, complete_down_weight = mlp_params(mlp_gain, w_gate, w_up, w_down)
    head_count = full_query.shape[1] // HEAD_SIZE
    kv_heads = full_key.shape[1] // HEAD_SIZE
    group_size = head_count // kv_heads
    residual = inputs.astype(jnp.float32)
    scale_one, unit_one = rms_stats(residual)
    normed_one = (unit_one * gain_one.astype(jnp.float32)).astype(jnp.bfloat16)
    normed_one_all = lax.all_gather(normed_one, "tensor", axis=0, tiled=True)
    query_full = jnp.dot(normed_one_all, full_query, preferred_element_type=jnp.float32).reshape(
        total_rows, head_count, HEAD_SIZE
    )
    queries = (
        rotate(query_full, cosine, sine_part, 1.0)
        .astype(jnp.bfloat16)
        .reshape(total_rows, kv_heads, group_size, HEAD_SIZE)
    )
    key_full = jnp.dot(normed_one_all, full_key, preferred_element_type=jnp.float32).reshape(
        total_rows, kv_heads, HEAD_SIZE
    )
    keys_rot = rotate(key_full, cosine, sine_part, 1.0).astype(jnp.bfloat16)
    values = jnp.dot(normed_one_all, full_value, preferred_element_type=jnp.float32).astype(
        jnp.bfloat16
    )
    values = values.reshape(total_rows, kv_heads, HEAD_SIZE)
    attended, log_total = attention_forward(queries, keys_rot, values, document_segment, QBLK)
    attended_flat = attended.reshape(total_rows, head_count * HEAD_SIZE)
    rows_part = attended_flat
    attn_out = lax.psum_scatter(
        jnp.dot(rows_part, full_output, preferred_element_type=jnp.float32),
        "tensor",
        scatter_dimension=0,
        tiled=True,
    )
    hidden = residual + valid_own * attn_out
    scale_two, unit_two = rms_stats(hidden)
    normed_two = (unit_two * gain_two.astype(jnp.float32)).astype(jnp.bfloat16)
    normed_two_all = lax.all_gather(normed_two, "tensor", axis=0, tiled=True)
    gate_pre = jnp.dot(normed_two_all, full_gate, preferred_element_type=jnp.float32)
    up_proj = jnp.dot(normed_two_all, full_up, preferred_element_type=jnp.float32)
    sigmoid_gate = jax.nn.sigmoid(gate_pre)
    activation = (gate_pre * sigmoid_gate * up_proj).astype(jnp.bfloat16)
    rows_part = activation
    mlp_out = lax.psum_scatter(
        jnp.dot(rows_part, complete_down_weight, preferred_element_type=jnp.float32),
        "tensor",
        scatter_dimension=0,
        tiled=True,
    )
    output = hidden + valid_own * mlp_out
    gain_one, full_query, full_key, full_value, full_output = attn_params(
        attn_gain, w_query, w_key, value_weight, w_output
    )
    gain_two, full_gate, full_up, complete_down_weight = mlp_params(mlp_gain, w_gate, w_up, w_down)
    grad_out = out_grad.astype(jnp.float32)
    grad_mlp = (grad_out * valid_own).astype(jnp.bfloat16)
    grad_mlp_all = lax.all_gather(grad_mlp, "tensor", axis=0, tiled=True)
    w_down_part = jnp.dot(activation.T, grad_mlp_all, preferred_element_type=jnp.float32)
    grad_act = jnp.dot(grad_mlp_all, complete_down_weight.T, preferred_element_type=jnp.float32)
    grad_gate = (
        grad_act * up_proj * sigmoid_gate * (1.0 + gate_pre * (1.0 - sigmoid_gate))
    ).astype(jnp.bfloat16)
    grad_up = (grad_act * gate_pre * sigmoid_gate).astype(jnp.bfloat16)
    grad_normed_two = lax.psum_scatter(
        jnp.dot(grad_gate, full_gate.T, preferred_element_type=jnp.float32)
        + jnp.dot(grad_up, full_up.T, preferred_element_type=jnp.float32),
        "tensor",
        scatter_dimension=0,
        tiled=True,
    )
    w_gate_part = jnp.dot(normed_two_all.T, grad_gate, preferred_element_type=jnp.float32)
    w_up_part = jnp.dot(normed_two_all.T, grad_up, preferred_element_type=jnp.float32)
    mlp_gain_part = jnp.sum(grad_normed_two * unit_two, axis=0)
    mlp_gain_slice, w_gate_grad, w_up_grad, w_down_grad = (
        lax.psum_scatter(mlp_gain_part, "dp", scatter_dimension=0, tiled=True),
        lax.psum_scatter(w_gate_part, "dp", scatter_dimension=0, tiled=True),
        lax.psum_scatter(w_up_part, "dp", scatter_dimension=0, tiled=True),
        lax.psum_scatter(w_down_part, "dp", scatter_dimension=1, tiled=True),
    )
    grad_hidden = grad_out + norm_backward(
        grad_normed_two, unit_two, scale_two, gain_two.astype(jnp.float32)
    )
    grad_attn = (grad_hidden * valid_own).astype(jnp.bfloat16)
    grad_attn_all = lax.all_gather(grad_attn, "tensor", axis=0, tiled=True)
    w_output_part = jnp.dot(attended_flat.T, grad_attn_all, preferred_element_type=jnp.float32)
    grad_attended = jnp.dot(
        grad_attn_all, full_output.T, preferred_element_type=jnp.float32
    ).astype(jnp.bfloat16)
    grad_attended = grad_attended.reshape(total_rows, kv_heads, group_size, HEAD_SIZE)
    query_grad, key_grad, value_grad = attention_backward(
        queries, keys_rot, values, attended, grad_attended, log_total, document_segment, QBLK
    )
    query_back = (
        rotate(query_grad, cosine, sine_part, -1.0)
        .astype(jnp.bfloat16)
        .reshape(total_rows, head_count * HEAD_SIZE)
    )
    key_back = (
        rotate(key_grad, cosine, sine_part, -1.0)
        .astype(jnp.bfloat16)
        .reshape(total_rows, kv_heads * HEAD_SIZE)
    )
    value_back = value_grad.astype(jnp.bfloat16).reshape(total_rows, kv_heads * HEAD_SIZE)
    grad_normed_one = lax.psum_scatter(
        jnp.dot(query_back, full_query.T, preferred_element_type=jnp.float32)
        + jnp.dot(key_back, full_key.T, preferred_element_type=jnp.float32)
        + jnp.dot(value_back, full_value.T, preferred_element_type=jnp.float32),
        "tensor",
        scatter_dimension=0,
        tiled=True,
    )
    w_query_part = jnp.dot(normed_one_all.T, query_back, preferred_element_type=jnp.float32)
    w_key_part = jnp.dot(normed_one_all.T, key_back, preferred_element_type=jnp.float32)
    w_value_part = jnp.dot(normed_one_all.T, value_back, preferred_element_type=jnp.float32)
    attn_gain_part = jnp.sum(grad_normed_one * unit_one, axis=0)
    attn_gain_slice, w_query_grad, w_key_grad, w_value_grad, w_output_grad = (
        lax.psum_scatter(attn_gain_part, "dp", scatter_dimension=0, tiled=True),
        lax.psum_scatter(w_query_part, "dp", scatter_dimension=0, tiled=True),
        lax.psum_scatter(w_key_part, "dp", scatter_dimension=0, tiled=True),
        lax.psum_scatter(w_value_part, "dp", scatter_dimension=0, tiled=True),
        lax.psum_scatter(w_output_part, "dp", scatter_dimension=1, tiled=True),
    )
    input_grad = grad_hidden + norm_backward(
        grad_normed_one, unit_one, scale_one, gain_one.astype(jnp.float32)
    )
    gain_sums = lax.psum((attn_gain_slice, mlp_gain_slice), "tensor")
    return (
        output,
        input_grad,
        gain_sums[0],
        w_query_grad,
        w_key_grad,
        w_value_grad,
        w_output_grad,
        gain_sums[1],
        w_gate_grad,
        w_up_grad,
        w_down_grad,
    )


def solution(mesh):
    placed = (
        P(("dp", "tensor"), None),
        P("dp", None),
        P("dp"),
        P("dp", "tensor"),
        P("dp", "tensor"),
        P("dp", "tensor"),
        P("tensor", "dp"),
        P("dp"),
        P("dp", "tensor"),
        P("dp", "tensor"),
        P("tensor", "dp"),
        P(("dp", "tensor"), None),
    )
    return jax.shard_map(
        per_device,
        mesh=mesh,
        in_specs=placed,
        out_specs=(
            P(("dp", "tensor"), None),
            P(("dp", "tensor"), None),
            P("dp"),
            P("dp", "tensor"),
            P("dp", "tensor"),
            P("dp", "tensor"),
            P("tensor", "dp"),
            P("dp"),
            P("dp", "tensor"),
            P("dp", "tensor"),
            P("tensor", "dp"),
        ),
        check_vma=False,
    )
```

profile of v0, /device:TPU:0, one launch (start us, length us, event | category | flops | bytes accessed | tf_op | source)
XLA Modules:
  0.0 1804.1 jit_solution(7006812651238048975)
XLA Ops:
  27.9 17.3 all_gather.51
  61.3 38.9 %all-gather.12.cloned.1.call-done = bf16[1024,2048]{1,0:T(8,128)(2,1)} async-done(((bf16[256,2048]{1,0:T(8,128)(2,1)}), bf16[1024,2048]{1,0:T(8,128)(2,1)}) %all-gather.12.cloned.1.call-update) | async-done | bytes 4194320 | tf_op jit(solution)/shard_map/all_gather | solution.py:185
  109.2 27.3 %while.27 = (s32[]{:T(128)}, bf16[2,512,2,4,64]{1,4,3,2,0:T(8,128)(2,1)S(1)}, f32[2,2,4,512]{3,2,1,0:T(4,128)S(1)}, s32[2]{0:T(128)S(1)}, s32[1024]{0:T(1024)S(1...) while((s32[]{:T(128)}, ...), condition=%wide.region_7.8_spmd, body=%wide.region_4.7_spmd.sunk | while | flops 1121710592 | bytes 54147264 | solution.py:81
  159.0 74.0 %reduce-scatter.12.cloned.1.call-done = f32[256,2048]{1,0:T(8,128)} async-done(((f32[1024,2048]{1,0:T(8,128)}), f32[256,2048]{1,0:T(8,128)}) %reduce-scatter.12.cloned.1.call-update) | async-done | bytes 2097168 | tf_op jit(solution)/shard_map/reduce_scatter | solution.py:205
  240.6 75.9 %all-gather.20.cloned.1.call-done = bf16[2048,2048]{1,0:T(8,128)(2,1)} async-done(((bf16[256,2048]{1,0:T(8,128)(2,1)}), bf16[2048,2048]{1,0:T(8,128)(2,1)}) %all-gather.20.cloned.1.call-update) | async-done | bytes 8388624 | tf_op jit(solution)/shard_map/all_gather | solution.py:148
  316.5 53.4 %all-gather.18.cloned.1.call-done = bf16[1024,2048]{1,0:T(8,128)(2,1)} async-done(((bf16[256,2048]{1,0:T(8,128)(2,1)}), bf16[1024,2048]{1,0:T(8,128)(2,1)}) %all-gather.18.cloned.1.call-update) | async-done | bytes 4194320 | tf_op jit(solution)/shard_map/all_gather | solution.py:214
  384.6 68.9 %all-gather.22.cloned.1.call-done = bf16[2048,2048]{1,0:T(8,128)(2,1)} async-done(((bf16[256,2048]{1,0:T(8,128)(2,1)}), bf16[2048,2048]{1,0:T(8,128)(2,1)}) %all-gather.22.cloned.1.call-update) | async-done | bytes 8388624 | tf_op jit(solution)/shard_map/all_gather | solution.py:149
  467.9 68.2 %all-gather.24.cloned.1.call-done = bf16[2048,2048]{1,0:T(8,128)(2,1)} async-done(((bf16[2048,256]{1,0:T(8,128)(2,1)}), bf16[2048,2048]{1,0:T(8,128)(2,1)}) %all-gather.24.cloned.1.call-update) | async-done | bytes 8388624 | tf_op jit(solution)/shard_map/all_gather | solution.py:150
  536.1 53.2 %all-gather.26.cloned.1.call-done = bf16[1024,2048]{1,0:T(8,128)(2,1)} async-done(((bf16[256,2048]{1,0:T(8,128)(2,1)}), bf16[1024,2048]{1,0:T(8,128)(2,1)}) %all-gather.26.cloned.1.call-update) | async-done | bytes 4194320 | tf_op jit(solution)/shard_map/all_gather | solution.py:233
  589.3 22.0 %multiply_convert_fusion = (bf16[1024,2048]{1,0:T(8,128)(2,1)}, bf16[1024,2048]{1,0:T(8,128)(2,1)}, bf16[1024,2048]{1,0:T(8,128)(2,1)}) fusion(f32[1024,2048]{1,0:T(8,128)} %fusion.71, f32[1024,2048]{1,0:T(8,128)} %fusion.72, bf16[1024,2048]{1,0:T(8,128)(2,1)} %all-gather.26.cloned.1.call-done, bf16[2048,2048]{1,0:T(8,128)(2,1)} %all-gather.24.cloned.1.call-done), kind=kOutput, calls=%fused_computation.62 | convolution fusion | flops 8623489024 | bytes 41943040 | tf_op jit(solution)/shard_map/dot_general | solution.py:235
  653.6 71.9 %reduce-scatter.16.cloned.1.call-done = f32[256,2048]{1,0:T(8,128)} async-done(((f32[1024,2048]{1,0:T(8,128)}), f32[256,2048]{1,0:T(8,128)}) %reduce-scatter.16.cloned.1.call-update) | async-done | bytes 2097168 | tf_op jit(solution)/shard_map/reduce_scatter | solution.py:240
  728.3 86.7 %reduce-scatter.14.cloned.1.call-done = f32[256,2048]{1,0:T(8,128)} async-done(((f32[1024,2048]{1,0:T(8,128)}), f32[256,2048]{1,0:T(8,128)}) %reduce-scatter.14.cloned.1.call-update) | async-done | bytes 2097168 | tf_op jit(solution)/shard_map/reduce_scatter | solution.py:220
  824.4 48.4 %all-gather.28.cloned.1.call-done = bf16[1024,2048]{1,0:T(8,128)(2,1)} async-done(((bf16[256,2048]{1,0:T(8,128)(2,1)}), bf16[1024,2048]{1,0:T(8,128)(2,1)}) %all-gather.28.cloned.1.call-update) | async-done | bytes 4194320 | tf_op jit(solution)/shard_map/all_gather | solution.py:260
  878.3 132.7 %while.28 = (s32[]{:T(128)}, f32[1024,2,64]{0,2,1:T(8,128)}, f32[1024,2,64]{0,2,1:T(8,128)}, f32[2,512,2,4,64]{1,0,4,3,2:T(2,128)}, s32[2]{0:T(128)S(1)}, /*inde...) while((s32[]{:T(128)}, f32[1024,2,64]{0,2,1:T(8,128)}, ...), condition=%wide.region_14.15_spmd.clone, body=%wide.region_13.14_spmd.clone.sunk | while | flops 2729832960 | bytes 146422416 | solution.py:129
  910.9 19.6 %dynamic_update_slice.20 = f32[2,512,2,4,64]{1,0,4,3,2:T(2,128)} dynamic-update-slice(f32[2,512,2,4,64]{1,0,4,3,2:T(2,128)} %get-tuple-element.421, f32[1,512,2,4,64]{1,0,4,3,2:T(1,128)S(1)} %copy.60, s32[]{:T(128)} %get-tuple-element.418, s32[]{:T(128)} %constant.45.clone.1..sunk.1, s32[]{:T(128)} %constant.45.clone.1..sunk.1, s32[]{:T(128)} %constant.45.clone.1..sunk.1, s32[]{:T(128)} %constant.45.clone.1..sunk.1) | dynamic-update-slice | bytes 2097156 | tf_op jit(solution)/shard_map/while/body/jit(dynamic_update_index_in_dim)/dynamic_update_slice | solution.py:129
  976.9 19.6 %dynamic_update_slice.20 = f32[2,512,2,4,64]{1,0,4,3,2:T(2,128)} dynamic-update-slice(f32[2,512,2,4,64]{1,0,4,3,2:T(2,128)} %get-tuple-element.421, f32[1,512,2,4,64]{1,0,4,3,2:T(1,128)S(1)} %copy.60, s32[]{:T(128)} %get-tuple-element.418, s32[]{:T(128)} %constant.45.clone.1..sunk.1, s32[]{:T(128)} %constant.45.clone.1..sunk.1, s32[]{:T(128)} %constant.45.clone.1..sunk.1, s32[]{:T(128)} %constant.45.clone.1..sunk.1) | dynamic-update-slice | bytes 2097156 | tf_op jit(solution)/shard_map/while/body/jit(dynamic_update_index_in_dim)/dynamic_update_slice | solution.py:129
  1070.5 15.5 fusion.82
  1119.8 28.5 %all-reduce.2 = (f32[2048]{0:T(1024)S(1)}, f32[2048]{0:T(1024)S(1)}) all-reduce(f32[2048]{0:T(1024)S(1)} %get-tuple-element.164, f32[2048]{0:T(1024)S(1)} %copy-done.33), channel_id=6, replica_groups=mesh['dp'=8,'tensor'=4] {'dp'}, use_global_device_ids=true, to_apply=%region_18.19.clone | all-reduce | flops 4096 | bytes 32768
  1163.0 23.4 %reduce-scatter.24.cloned.1.call-done = f32[256,128]{1,0:T(8,128)} async-done(((f32[2048,128]{1,0:T(8,128)}), f32[256,128]{1,0:T(8,128)}) %reduce-scatter.24.cloned.1.call-update) | async-done | bytes 131088 | tf_op jit(solution)/shard_map/reduce_scatter | solution.py:296
  1186.4 50.8 %reduce-scatter.20.cloned.1.call-done = f32[256,512]{1,0:T(8,128)} async-done(((f32[2048,512]{1,0:T(8,128)}), f32[256,512]{1,0:T(8,128)}) %reduce-scatter.20.cloned.1.call-update) | async-done | bytes 524304 | tf_op jit(solution)/shard_map/reduce_scatter | solution.py:294
  1237.3 51.1 %reduce-scatter.26.cloned.1.call-done = f32[512,256]{1,0:T(8,128)} async-done(((f32[512,2048]{1,0:T(8,128)}), f32[512,256]{1,0:T(8,128)}) %reduce-scatter.26.cloned.1.call-update) | async-done | bytes 524304 | tf_op jit(solution)/shard_map/reduce_scatter | solution.py:297
  1288.4 169.5 %reduce-scatter.28.cloned.1.call-done = f32[256,2048]{1,0:T(8,128)} async-done(((f32[2048,2048]{1,0:T(8,128)}), f32[256,2048]{1,0:T(8,128)}) %reduce-scatter.28.cloned.1.call-update) | async-done | bytes 2097168 | tf_op jit(solution)/shard_map/reduce_scatter | solution.py:252
  1457.8 169.6 %reduce-scatter.30.cloned.1.call-done = f32[256,2048]{1,0:T(8,128)} async-done(((f32[2048,2048]{1,0:T(8,128)}), f32[256,2048]{1,0:T(8,128)}) %reduce-scatter.30.cloned.1.call-update) | async-done | bytes 2097168 | tf_op jit(solution)/shard_map/reduce_scatter | solution.py:253
  1627.4 169.4 %reduce-scatter.32.cloned.1.call-done = f32[2048,256]{1,0:T(8,128)} async-done(((f32[2048,2048]{1,0:T(8,128)}), f32[2048,256]{1,0:T(8,128)}) %reduce-scatter.32.cloned.1.call-update) | async-done | bytes 2097168 | tf_op jit(solution)/shard_map/reduce_scatter | solution.py:254
  (282 shorter events, 384.4 us)
Async XLA Ops:
  7.2 54.1 %all-gather.14.cloned.1.call-start = ((), (), s32[]{:S(2)}) async-start(), calls=%async_computation.12 | async-start | bytes 2359296 | tf_op jit(solution)/shard_map/all_gather | solution.py:138
  7.9 92.2 %all-gather.12.cloned.1.call-start = ((), (), s32[]{:S(2)}) async-start(), calls=%async_computation.11 | async-start | bytes 5242880 | tf_op jit(solution)/shard_map/all_gather | solution.py:185
  26.8 112.1 %all-gather.16.cloned.1.call-start = ((), (), s32[]{:S(2)}) async-start(), calls=%async_computation.13 | async-start | bytes 2359296 | tf_op jit(solution)/shard_map/all_gather | solution.py:141
  27.5 205.4 %reduce-scatter.12.cloned.1.call-start = ((), (), s32[]{:S(2)}) async-start(), calls=%async_computation.14 | async-start | bytes 10485760 | tf_op jit(solution)/shard_map/reduce_scatter | solution.py:205
  146.5 170.0 %all-gather.20.cloned.1.call-start = ((), (), s32[]{:S(2)}) async-start(), calls=%async_computation.16 | async-start | bytes 9437184 | tf_op jit(solution)/shard_map/all_gather | solution.py:148
  147.1 222.8 %all-gather.18.cloned.1.call-start = ((), (), s32[]{:S(2)}) async-start(), calls=%async_computation.15 | async-start | bytes 5242880 | tf_op jit(solution)/shard_map/all_gather | solution.py:214
  158.9 656.1 %copy-start.27 = (f32[8,1,256]{2,1,0:T(1,128)}, f32[8,1,256]{2,1,0:T(1,128)S(1)}, u32[]{:S(2)}) copy-start(f32[8,1,256]{2,1,0:T(1,128)S(1)} %convert_element_type.105) | copy-start | bytes 24580
  236.7 578.2 %copy-start.8 = (f32[256,2048]{1,0:T(8,128)}, f32[256,2048]{1,0:T(8,128)S(1)}, u32[]{:S(2)}) copy-start(f32[256,2048]{1,0:T(8,128)S(1)} %get-tuple-element.215) | copy-start | bytes 6291460
  236.7 578.2 %copy-start.34 = (f32[256]{0:T(256)}, f32[256]{0:T(256)S(1)}, u32[]{:S(2)}) copy-start(f32[256]{0:T(256)S(1)} %add_rsqrt_fusion) | copy-start | bytes 3076
  238.3 215.2 %all-gather.22.cloned.1.call-start = ((), (), s32[]{:S(2)}) async-start(), calls=%async_computation.17 | async-start | bytes 9437184 | tf_op jit(solution)/shard_map/all_gather | solution.py:149
  239.0 297.0 %all-gather.24.cloned.1.call-start = ((), (), s32[]{:S(2)}) async-start(), calls=%async_computation.18 | async-start | bytes 9437184 | tf_op jit(solution)/shard_map/all_gather | solution.py:150
  239.8 349.5 %all-gather.26.cloned.1.call-start = ((), (), s32[]{:S(2)}) async-start(), calls=%async_computation.20 | async-start | bytes 5242880 | tf_op jit(solution)/shard_map/all_gather | solution.py:233
  240.5 485.0 %reduce-scatter.16.cloned.1.call-start = ((), (), s32[]{:S(2)}) async-start(), calls=%async_computation.21 | async-start | bytes 10485760 | tf_op jit(solution)/shard_map/reduce_scatter | solution.py:240
  639.0 175.9 %reduce-scatter.14.cloned.1.call-start = ((), (), s32[]{:S(2)}) async-start(), calls=%async_computation.19 | async-start | bytes 10485760 | tf_op jit(solution)/shard_map/reduce_scatter | solution.py:220
  653.6 219.2 %all-gather.28.cloned.1.call-start = ((), (), s32[]{:S(2)}) async-start(), calls=%async_computation.22 | async-start | bytes 5242880 | tf_op jit(solution)/shard_map/all_gather | solution.py:260
  820.1 297.5 %reduce-scatter.18.cloned.1.call-start = ((), (), s32[]{:S(2)}) async-start(), calls=%async_computation.23 | async-start | bytes 10485760 | tf_op jit(solution)/shard_map/reduce_scatter | solution.py:280
  878.3 132.7 %copy-start.17 = (f32[1024,32]{0,1:T(8,128)S(1)}, f32[1024,32]{0,1:T(8,128)}, u32[]{:S(2)}) copy-start(f32[1024,32]{0,1:T(8,128)} %copy-done.16) | copy-start | bytes 393220
  1031.1 131.9 %reduce-scatter.22.cloned.1.call-start = ((), (), s32[]{:S(2)}) async-start(), calls=%async_computation.25 | async-start | bytes 1179648 | tf_op jit(solution)/shard_map/reduce_scatter | solution.py:295
  1035.6 150.8 %reduce-scatter.24.cloned.1.call-start = ((), (), s32[]{:S(2)}) async-start(), calls=%async_computation.26 | async-start | bytes 1179648 | tf_op jit(solution)/shard_map/reduce_scatter | solution.py:296
  1040.3 197.0 %reduce-scatter.20.cloned.1.call-start = ((), (), s32[]{:S(2)}) async-start(), calls=%async_computation.24 | async-start | bytes 4718592 | tf_op jit(solution)/shard_map/reduce_scatter | solution.py:294
  1047.0 241.3 %reduce-scatter.26.cloned.1.call-start = ((), (), s32[]{:S(2)}) async-start(), calls=%async_computation.27 | async-start | bytes 4718592 | tf_op jit(solution)/shard_map/reduce_scatter | solution.py:297
  1055.0 402.9 %reduce-scatter.28.cloned.1.call-start = ((), (), s32[]{:S(2)}) async-start(), calls=%async_computation.28 | async-start | bytes 18874368 | tf_op jit(solution)/shard_map/reduce_scatter | solution.py:252
  1070.4 557.0 %reduce-scatter.30.cloned.1.call-start = ((), (), s32[]{:S(2)}) async-start(), calls=%async_computation.29 | async-start | bytes 18874368 | tf_op jit(solution)/shard_map/reduce_scatter | solution.py:253
  1086.0 710.9 %reduce-scatter.32.cloned.1.call-start = ((), (), s32[]{:S(2)}) async-start(), calls=%async_computation.30 | async-start | bytes 18874368 | tf_op jit(solution)/shard_map/reduce_scatter | solution.py:254
  (57 other events, 1034.8 us)
Sparse Core Ops, SparseCore 0:
  9.6 36.1 all-gather.13
  48.3 51.8 all-gather.11
  101.7 30.5 all-gather.15
  146.6 86.3 reduce-scatter.11
  234.4 82.0 all-gather.19
  318.7 51.0 all-gather.17
  371.4 82.0 all-gather.21
  455.1 80.9 all-gather.23
  538.5 50.7 all-gather.25
  639.2 86.3 reduce-scatter.15
  728.6 86.3 reduce-scatter.13
  820.2 52.5 all-gather.27
  1031.2 86.3 reduce-scatter.17
  1120.2 32.5 reduce-scatter.21
  1155.6 30.8 reduce-scatter.23
  1189.1 48.0 reduce-scatter.19
  1240.0 48.3 reduce-scatter.25
  1291.2 166.6 reduce-scatter.27
  1460.8 166.6 reduce-scatter.29
  1630.2 166.6 reduce-scatter.31
where the time goes:
time: 1810 us; the launch traced here: 1800 us
  waiting for transfers between devices  1290 us (71%)
  matrix products  281 us (16%)
  blocking collectives  95.4 us (5%)
  local copies, waits for them, and re-layouts  61.6 us (3%)
  other arithmetic  49.3 us (3%)
    reduce_scatter x1, waiting for transfers between devices, per_device(): lax.psum_scatter(w_up_part, 'dp', scatter_dimension=0, tiled=True)  170 us
    reduce_scatter x1, waiting for transfers between devices, per_device(): lax.psum_scatter(w_gate_part, 'dp', scatter_dimension=0, tiled=True)  169 us
    reduce_scatter x1, waiting for transfers between devices, per_device(): lax.psum_scatter(w_down_part, 'dp', scatter_dimension=1, tiled=True)  169 us
    reduce_scatter x1, waiting for transfers between devices, per_device(): lax.psum_scatter(jnp.dot(rows_part, complete_down_weight, preferred_eleme...  86.7 us
    all_gather x1, waiting for transfers between devices, mlp_params(): lax.all_gather(w_gate, 'dp', axis=0, tiled=True)  75.9 us
    reduce_scatter x1, waiting for transfers between devices, per_device(): lax.psum_scatter(jnp.dot(rows_part, full_output, preferred_element_type=j...  74 us
    reduce_scatter x1, waiting for transfers between devices, per_device(): lax.psum_scatter(jnp.dot(grad_gate, full_gate.T, preferred_element_type=j...  71.9 us
    all_gather x1, waiting for transfers between devices, mlp_params(): lax.all_gather(w_up, 'dp', axis=0, tiled=True)  68.9 us
  transfers between devices with their start and end apart: 20, of which 17 were waited for; matrix products, arithmetic and copies ran while one was open for 10% of the time, Pallas kernels for 0%

commit v1 on v0

--- a/solution.py
+++ b/solution.py
@@ -211,7 +211,9 @@
     hidden = residual + valid_own * attn_out
     scale_two, unit_two = rms_stats(hidden)
     normed_two = (unit_two * gain_two.astype(jnp.float32)).astype(jnp.bfloat16)
-    normed_two_all = lax.all_gather(normed_two, "tensor", axis=0, tiled=True)
+    normed_two_all = jnp.concatenate(
+        lax.all_to_all(jnp.stack([normed_two] * lax.axis_size("tensor")), "tensor", 0, 0), axis=0
+    )
     gate_pre = jnp.dot(normed_two_all, full_gate, preferred_element_type=jnp.float32)
     up_proj = jnp.dot(normed_two_all, full_up, preferred_element_type=jnp.float32)
     sigmoid_gate = jax.nn.sigmoid(gate_pre)

time: 1810 us -> 1760 us (0.972)
  waiting for transfers between devices: 1290 us -> 1230 us
    all_gather x1 -> x0, waiting for transfers between devices: 53.4 us -> none  [per_device(): normed_two_all = lax.all_gather(normed_two, 'tensor', axis=0, tiled=True)]
  transfers between devices with their start and end apart: 20 -> 20, of which waited for: 17 -> 16; matrix products, arithmetic and copies ran while one was open for 10% -> 10% of each run, Pallas kernels for 0% -> 0%
where the time goes in v1:
time: 1760 us; the launch traced here: 1750 us
  waiting for transfers between devices  1230 us (70%)
  matrix products  278 us (16%)
  blocking collectives  95.5 us (5%)
  local copies, waits for them, and re-layouts  66.2 us (4%)
  other arithmetic  47.2 us (3%)
    reduce_scatter x1, waiting for transfers between devices, per_device(): lax.psum_scatter(w_down_part, 'dp', scatter_dimension=1, tiled=True)  170 us
    reduce_scatter x1, waiting for transfers between devices, per_device(): lax.psum_scatter(w_up_part, 'dp', scatter_dimension=0, tiled=True)  169 us
    reduce_scatter x1, waiting for transfers between devices, per_device(): lax.psum_scatter(w_gate_part, 'dp', scatter_dimension=0, tiled=True)  169 us
    reduce_scatter x1, waiting for transfers between devices, per_device(): lax.psum_scatter(jnp.dot(rows_part, complete_down_weight, preferred_eleme...  86.5 us
    reduce_scatter x1, waiting for transfers between devices, per_device(): lax.psum_scatter(jnp.dot(rows_part, full_output, preferred_element_type=j...  72.7 us
    reduce_scatter x1, waiting for transfers between devices, per_device(): lax.psum_scatter(jnp.dot(grad_gate, full_gate.T, preferred_element_type=j...  71.9 us
    all_gather x1, waiting for transfers between devices, mlp_params(): lax.all_gather(w_gate, 'dp', axis=0, tiled=True)  71.4 us
    all_gather x1, waiting for transfers between devices, mlp_params(): lax.all_gather(w_down, 'dp', axis=1, tiled=True)  68.1 us
  transfers between devices with their start and end apart: 20, of which 16 were waited for; matrix products, arithmetic and copies ran while one was open for 10% of the time, Pallas kernels for 0%

profile of v1, /device:TPU:0, one launch (start us, length us, event | category | flops | bytes accessed | tf_op | source)
XLA Modules:
  0.0 1747.6 jit_solution(6626544312912468454)
XLA Ops:
  27.9 17.3 all_gather.48
  61.3 38.9 %all-gather.11.cloned.1.call-done = bf16[1024,2048]{1,0:T(8,128)(2,1)} async-done(((bf16[256,2048]{1,0:T(8,128)(2,1)}), bf16[1024,2048]{1,0:T(8,128)(2,1)}) %all-gather.11.cloned.1.call-update) | async-done | bytes 4194320 | tf_op jit(solution)/shard_map/all_gather | solution.py:185
  109.2 27.3 %while.27 = (s32[]{:T(128)}, bf16[2,512,2,4,64]{1,4,3,2,0:T(8,128)(2,1)S(1)}, f32[2,2,4,512]{3,2,1,0:T(4,128)S(1)}, s32[2]{0:T(128)S(1)}, s32[1024]{0:T(1024)S(1...) while((s32[]{:T(128)}, ...), condition=%wide.region_7.8_spmd, body=%wide.region_4.7_spmd.sunk | while | flops 1121710592 | bytes 54147264 | solution.py:81
  160.3 72.7 %reduce-scatter.12.cloned.1.call-done = f32[256,2048]{1,0:T(8,128)} async-done(((f32[1024,2048]{1,0:T(8,128)}), f32[256,2048]{1,0:T(8,128)}) %reduce-scatter.12.cloned.1.call-update) | async-done | bytes 2097168 | tf_op jit(solution)/shard_map/reduce_scatter | solution.py:205
  245.2 71.4 %all-gather.17.cloned.1.call-done = bf16[2048,2048]{1,0:T(8,128)(2,1)} async-done(((bf16[256,2048]{1,0:T(8,128)(2,1)}), bf16[2048,2048]{1,0:T(8,128)(2,1)}) %all-gather.17.cloned.1.call-update) | async-done | bytes 8388624 | tf_op jit(solution)/shard_map/all_gather | solution.py:148
  331.3 67.2 %all-gather.19.cloned.1.call-done = bf16[2048,2048]{1,0:T(8,128)(2,1)} async-done(((bf16[256,2048]{1,0:T(8,128)(2,1)}), bf16[2048,2048]{1,0:T(8,128)(2,1)}) %all-gather.19.cloned.1.call-update) | async-done | bytes 8388624 | tf_op jit(solution)/shard_map/all_gather | solution.py:149
  413.0 68.1 %all-gather.21.cloned.1.call-done = bf16[2048,2048]{1,0:T(8,128)(2,1)} async-done(((bf16[2048,256]{1,0:T(8,128)(2,1)}), bf16[2048,2048]{1,0:T(8,128)(2,1)}) %all-gather.21.cloned.1.call-update) | async-done | bytes 8388624 | tf_op jit(solution)/shard_map/all_gather | solution.py:150
  481.1 53.2 %all-gather.23.cloned.1.call-done = bf16[1024,2048]{1,0:T(8,128)(2,1)} async-done(((bf16[256,2048]{1,0:T(8,128)(2,1)}), bf16[1024,2048]{1,0:T(8,128)(2,1)}) %all-gather.23.cloned.1.call-update) | async-done | bytes 4194320 | tf_op jit(solution)/shard_map/all_gather | solution.py:235
  534.3 22.0 %multiply_convert_fusion = (bf16[1024,2048]{1,0:T(8,128)(2,1)}, bf16[1024,2048]{1,0:T(8,128)(2,1)}, bf16[1024,2048]{1,0:T(8,128)(2,1)}) fusion(f32[1024,2048]{1,0:T(8,128)} %fusion.71, f32[1024,2048]{1,0:T(8,128)} %fusion.72, bf16[1024,2048]{1,0:T(8,128)(2,1)} %all-gather.23.cloned.1.call-done, bf16[2048,2048]{1,0:T(8,128)(2,1)} %all-gather.21.cloned.1.call-done), kind=kOutput, calls=%fused_computation.62 | convolution fusion | flops 8623489024 | bytes 41943040 | tf_op jit(solution)/shard_map/dot_general | solution.py:237
  598.7 71.9 %reduce-scatter.16.cloned.1.call-done = f32[256,2048]{1,0:T(8,128)} async-done(((f32[1024,2048]{1,0:T(8,128)}), f32[256,2048]{1,0:T(8,128)}) %reduce-scatter.16.cloned.1.call-update) | async-done | bytes 2097168 | tf_op jit(solution)/shard_map/reduce_scatter | solution.py:242
  673.3 86.5 %reduce-scatter.14.cloned.1.call-done = f32[256,2048]{1,0:T(8,128)} async-done(((f32[1024,2048]{1,0:T(8,128)}), f32[256,2048]{1,0:T(8,128)}) %reduce-scatter.14.cloned.1.call-update) | async-done | bytes 2097168 | tf_op jit(solution)/shard_map/reduce_scatter | solution.py:222
  768.8 48.6 %all-gather.25.cloned.1.call-done = bf16[1024,2048]{1,0:T(8,128)(2,1)} async-done(((bf16[256,2048]{1,0:T(8,128)(2,1)}), bf16[1024,2048]{1,0:T(8,128)(2,1)}) %all-gather.25.cloned.1.call-update) | async-done | bytes 4194320 | tf_op jit(solution)/shard_map/all_gather | solution.py:262
  822.7 131.8 %while.28 = (s32[]{:T(128)}, f32[1024,2,64]{0,2,1:T(8,128)}, f32[1024,2,64]{0,2,1:T(8,128)}, f32[2,512,2,4,64]{1,0,4,3,2:T(2,128)}, s32[2]{0:T(128)S(1)}, /*inde...) while((s32[]{:T(128)}, f32[1024,2,64]{0,2,1:T(8,128)}, ...), condition=%wide.region_14.15_spmd.clone, body=%wide.region_13.14_spmd.clone.sunk | while | flops 2729832960 | bytes 148519536 | solution.py:129
  854.9 19.6 %dynamic_update_slice.20 = f32[2,512,2,4,64]{1,0,4,3,2:T(2,128)} dynamic-update-slice(f32[2,512,2,4,64]{1,0,4,3,2:T(2,128)} %get-tuple-element.421, f32[1,512,2,4,64]{1,0,4,3,2:T(1,128)S(1)} %copy.60, s32[]{:T(128)} %get-tuple-element.418, s32[]{:T(128)} %constant.45.clone.1..sunk.1, s32[]{:T(128)} %constant.45.clone.1..sunk.1, s32[]{:T(128)} %constant.45.clone.1..sunk.1, s32[]{:T(128)} %constant.45.clone.1..sunk.1) | dynamic-update-slice | bytes 2097156 | tf_op jit(solution)/shard_map/while/body/jit(dynamic_update_index_in_dim)/dynamic_update_slice | solution.py:129
  920.5 19.6 %dynamic_update_slice.20 = f32[2,512,2,4,64]{1,0,4,3,2:T(2,128)} dynamic-update-slice(f32[2,512,2,4,64]{1,0,4,3,2:T(2,128)} %get-tuple-element.421, f32[1,512,2,4,64]{1,0,4,3,2:T(1,128)S(1)} %copy.60, s32[]{:T(128)} %get-tuple-element.418, s32[]{:T(128)} %constant.45.clone.1..sunk.1, s32[]{:T(128)} %constant.45.clone.1..sunk.1, s32[]{:T(128)} %constant.45.clone.1..sunk.1, s32[]{:T(128)} %constant.45.clone.1..sunk.1) | dynamic-update-slice | bytes 2097156 | tf_op jit(solution)/shard_map/while/body/jit(dynamic_update_index_in_dim)/dynamic_update_slice | solution.py:129
  998.5 15.4 fusion.81
  1014.0 15.5 fusion.82
  1063.2 28.6 %all-reduce.2 = (f32[2048]{0:T(1024)S(1)}, f32[2048]{0:T(1024)S(1)}) all-reduce(f32[2048]{0:T(1024)S(1)} %get-tuple-element.164, f32[2048]{0:T(1024)S(1)} %copy-done.37), channel_id=6, replica_groups=mesh['dp'=8,'tensor'=4] {'dp'}, use_global_device_ids=true, to_apply=%region_18.19.clone | all-reduce | flops 4096 | bytes 32768
  1106.6 23.6 %reduce-scatter.24.cloned.1.call-done = f32[256,128]{1,0:T(8,128)} async-done(((f32[2048,128]{1,0:T(8,128)}), f32[256,128]{1,0:T(8,128)}) %reduce-scatter.24.cloned.1.call-update) | async-done | bytes 131088 | tf_op jit(solution)/shard_map/reduce_scatter | solution.py:298
  1130.1 50.9 %reduce-scatter.20.cloned.1.call-done = f32[256,512]{1,0:T(8,128)} async-done(((f32[2048,512]{1,0:T(8,128)}), f32[256,512]{1,0:T(8,128)}) %reduce-scatter.20.cloned.1.call-update) | async-done | bytes 524304 | tf_op jit(solution)/shard_map/reduce_scatter | solution.py:296
  1181.1 51.1 %reduce-scatter.26.cloned.1.call-done = f32[512,256]{1,0:T(8,128)} async-done(((f32[512,2048]{1,0:T(8,128)}), f32[512,256]{1,0:T(8,128)}) %reduce-scatter.26.cloned.1.call-update) | async-done | bytes 524304 | tf_op jit(solution)/shard_map/reduce_scatter | solution.py:299
  1232.2 169.4 %reduce-scatter.28.cloned.1.call-done = f32[256,2048]{1,0:T(8,128)} async-done(((f32[2048,2048]{1,0:T(8,128)}), f32[256,2048]{1,0:T(8,128)}) %reduce-scatter.28.cloned.1.call-update) | async-done | bytes 2097168 | tf_op jit(solution)/shard_map/reduce_scatter | solution.py:254
  1401.6 169.4 %reduce-scatter.30.cloned.1.call-done = f32[256,2048]{1,0:T(8,128)} async-done(((f32[2048,2048]{1,0:T(8,128)}), f32[256,2048]{1,0:T(8,128)}) %reduce-scatter.30.cloned.1.call-update) | async-done | bytes 2097168 | tf_op jit(solution)/shard_map/reduce_scatter | solution.py:255
  1571.1 169.6 %reduce-scatter.32.cloned.1.call-done = f32[2048,256]{1,0:T(8,128)} async-done(((f32[2048,2048]{1,0:T(8,128)}), f32[2048,256]{1,0:T(8,128)}) %reduce-scatter.32.cloned.1.call-update) | async-done | bytes 2097168 | tf_op jit(solution)/shard_map/reduce_scatter | solution.py:256
  (286 shorter events, 373.3 us)
Async XLA Ops:
  7.2 54.1 %all-gather.13.cloned.1.call-start = ((), (), s32[]{:S(2)}) async-start(), calls=%async_computation.13 | async-start | bytes 2359296 | tf_op jit(solution)/shard_map/all_gather | solution.py:138
  7.9 92.2 %all-gather.11.cloned.1.call-start = ((), (), s32[]{:S(2)}) async-start(), calls=%async_computation.12 | async-start | bytes 5242880 | tf_op jit(solution)/shard_map/all_gather | solution.py:185
  26.8 112.1 %all-gather.15.cloned.1.call-start = ((), (), s32[]{:S(2)}) async-start(), calls=%async_computation.14 | async-start | bytes 2359296 | tf_op jit(solution)/shard_map/all_gather | solution.py:141
  27.5 205.5 %reduce-scatter.12.cloned.1.call-start = ((), (), s32[]{:S(2)}) async-start(), calls=%async_computation.15 | async-start | bytes 10485760 | tf_op jit(solution)/shard_map/reduce_scatter | solution.py:205
  146.5 170.0 %all-gather.17.cloned.1.call-start = ((), (), s32[]{:S(2)}) async-start(), calls=%async_computation.16 | async-start | bytes 9437184 | tf_op jit(solution)/shard_map/all_gather | solution.py:148
  147.1 251.4 %all-gather.19.cloned.1.call-start = ((), (), s32[]{:S(2)}) async-start(), calls=%async_computation.17 | async-start | bytes 9437184 | tf_op jit(solution)/shard_map/all_gather | solution.py:149
  147.7 333.4 %all-gather.21.cloned.1.call-start = ((), (), s32[]{:S(2)}) async-start(), calls=%async_computation.18 | async-start | bytes 9437184 | tf_op jit(solution)/shard_map/all_gather | solution.py:150
  160.2 599.6 %copy-start.31 = (f32[8,1,256]{2,1,0:T(1,128)}, f32[8,1,256]{2,1,0:T(1,128)S(1)}, u32[]{:S(2)}) copy-start(f32[8,1,256]{2,1,0:T(1,128)S(1)} %convert_element_type.105) | copy-start | bytes 24580
  236.5 523.4 %copy-start.8 = (f32[256,2048]{1,0:T(8,128)}, f32[256,2048]{1,0:T(8,128)S(1)}, u32[]{:S(2)}) copy-start(f32[256,2048]{1,0:T(8,128)S(1)} %get-tuple-element.215) | copy-start | bytes 6291460
  236.5 523.4 %copy-start.38 = (f32[256]{0:T(256)}, f32[256]{0:T(256)S(1)}, u32[]{:S(2)}) copy-start(f32[256]{0:T(256)S(1)} %add_rsqrt_fusion) | copy-start | bytes 3076
  239.4 77.1 %all-to-all-start = ((bf16[4,256,2048]{2,1,0:T(8,128)(2,1)}), bf16[4,256,2048]{2,1,0:T(8,128)(2,1)}, u32[]{:S(2)}, u32[]{:S(2)}) async-start(bf16[4,256,2048]{2,1,0:T(8,128)(2,1)} %stack.2), calls=%async_computation.1 | async-start | bytes 8388608 | tf_op jit(solution)/shard_map/all_to_all | solution.py:215
  244.4 290.0 %all-gather.23.cloned.1.call-start = ((), (), s32[]{:S(2)}) async-start(), calls=%async_computation.20 | async-start | bytes 5242880 | tf_op jit(solution)/shard_map/all_gather | solution.py:235
  245.1 425.5 %reduce-scatter.16.cloned.1.call-start = ((), (), s32[]{:S(2)}) async-start(), calls=%async_computation.21 | async-start | bytes 10485760 | tf_op jit(solution)/shard_map/reduce_scatter | solution.py:242
  584.1 175.7 %reduce-scatter.14.cloned.1.call-start = ((), (), s32[]{:S(2)}) async-start(), calls=%async_computation.19 | async-start | bytes 10485760 | tf_op jit(solution)/shard_map/reduce_scatter | solution.py:222
  598.7 161.2 %copy-start.12 = (bf16[256,2048]{1,0:T(8,128)(2,1)S(1)}, bf16[256,2048]{1,0:T(8,128)(2,1)}, u32[]{:S(2)}) copy-start(bf16[256,2048]{1,0:T(8,128)(2,1)} %param.27) | copy-start | bytes 3145732
  598.7 218.7 %all-gather.25.cloned.1.call-start = ((), (), s32[]{:S(2)}) async-start(), calls=%async_computation.22 | async-start | bytes 5242880 | tf_op jit(solution)/shard_map/all_gather | solution.py:262
  764.7 296.3 %reduce-scatter.18.cloned.1.call-start = ((), (), s32[]{:S(2)}) async-start(), calls=%async_computation.23 | async-start | bytes 10485760 | tf_op jit(solution)/shard_map/reduce_scatter | solution.py:282
  974.5 132.1 %reduce-scatter.22.cloned.1.call-start = ((), (), s32[]{:S(2)}) async-start(), calls=%async_computation.25 | async-start | bytes 1179648 | tf_op jit(solution)/shard_map/reduce_scatter | solution.py:297
  979.0 151.1 %reduce-scatter.24.cloned.1.call-start = ((), (), s32[]{:S(2)}) async-start(), calls=%async_computation.26 | async-start | bytes 1179648 | tf_op jit(solution)/shard_map/reduce_scatter | solution.py:298
  983.7 197.4 %reduce-scatter.20.cloned.1.call-start = ((), (), s32[]{:S(2)}) async-start(), calls=%async_computation.24 | async-start | bytes 4718592 | tf_op jit(solution)/shard_map/reduce_scatter | solution.py:296
  990.5 241.7 %reduce-scatter.26.cloned.1.call-start = ((), (), s32[]{:S(2)}) async-start(), calls=%async_computation.27 | async-start | bytes 4718592 | tf_op jit(solution)/shard_map/reduce_scatter | solution.py:299
  998.4 403.2 %reduce-scatter.28.cloned.1.call-start = ((), (), s32[]{:S(2)}) async-start(), calls=%async_computation.28 | async-start | bytes 18874368 | tf_op jit(solution)/shard_map/reduce_scatter | solution.py:254
  1013.9 557.2 %reduce-scatter.30.cloned.1.call-start = ((), (), s32[]{:S(2)}) async-start(), calls=%async_computation.29 | async-start | bytes 18874368 | tf_op jit(solution)/shard_map/reduce_scatter | solution.py:255
  1029.5 711.2 %reduce-scatter.32.cloned.1.call-start = ((), (), s32[]{:S(2)}) async-start(), calls=%async_computation.30 | async-start | bytes 18874368 | tf_op jit(solution)/shard_map/reduce_scatter | solution.py:256
  (59 other events, 1250.8 us)
Sparse Core Ops, SparseCore 0:
  9.6 36.1 all-gather.12
  48.3 51.8 all-gather.10
  101.7 30.5 all-gather.14
  146.7 86.3 reduce-scatter.11
  234.5 82.0 all-gather.16
  318.0 80.5 all-gather.18
  400.1 80.9 all-gather.20
  483.5 50.7 all-gather.22
  584.3 86.2 reduce-scatter.15
  673.5 86.3 reduce-scatter.13
  764.8 52.5 all-gather.24
  974.6 86.3 reduce-scatter.17
  1063.8 32.4 reduce-scatter.21
  1099.0 31.0 reduce-scatter.23
  1132.8 48.1 reduce-scatter.19
  1183.8 48.3 reduce-scatter.25
  1235.0 166.6 reduce-scatter.27
  1404.4 166.6 reduce-scatter.29
  1574.0 166.6 reduce-scatter.31
